TPU v7x, 128 devices: a whole 4x4x4 slice. The times are simulated.
128 devices in a mesh: grp: 4 (over z), tile: 32 (over x, y, core).
Axes of the slice: x: 4, y: 4, z: 4, core: 2. Of those that a mesh axis runs over, the one named last changes fastest.
Arguments:
- noise: bfloat16 [16, 3, 2048, 2048], P('grp', None, 'tile'), may hold values from -6 to 6
- stress: float32 [6, 2048, 2048], P(None, 'tile', 'grp'), as said below
- timescale: float32 [2048, 2048], P('tile', 'grp'), may hold values from 3 to 256
- mean_inflow: float32 [2048, 2048], P('tile', 'grp'), may hold values from 0.5 to 1.5
- courant: float32 [2048, 2048], P('tile', 'grp'), may hold values from 0.2 to 0.9
- prior_state: float32 [3, 2048, 2048], P(None, 'tile', 'grp'), may hold values from -6 to 6
- field: float32 [3, 8, 2048, 2048], P(None, None, 'tile', 'grp'), may hold values from -6 to 6
Outputs:
- inflow: bfloat16 [16, 3, 2048, 2048], P(None, None, 'tile', 'grp')
- field_out: float32 [3, 8, 2048, 2048], P(None, None, 'tile', 'grp')
Inputs may be any that keep to these rules, and one draw needn't show every extreme that they name: stress holds, per cell, R11, R21, R22, R31, R32, R33 of a symmetric positive definite tensor whose Cholesky factor has diagonal entries of 0.3 or more.
All inputs are finite; a program needn't handle non-finite values.
Results may differ from a plain program's by a relative error of at most 0.0085.
Values may be sent and summed in bfloat16 or wider, within the bound.
A program may use at most 128 MiB of HBM per device.

v0:
```python
import math
import jax
import jax.numpy as jnp
from jax import lax
from jax.sharding import PartitionSpec as P

LS = 2
FW = 4


def padded_2(value, sides, width, wrap):
    for axis, dim in sides:
        devices, length = (lax.axis_size(axis), value.shape[dim])
        up = [(i, (i + 1) % devices) for i in range(devices if wrap else devices - 1)]
        down = [(j, i) for i, j in up]
        last = lax.slice_in_dim(value, length - width, length, axis=dim)
        initial = lax.slice_in_dim(value, 0, width, axis=dim)
        before = lax.ppermute(last, axis, up)
        after = lax.ppermute(initial, axis, down)
        value = jnp.concatenate([before, value, after], axis=dim)
    return value


def filter_taps():
    offsets = jnp.arange(-FW, FW + 1).astype(jnp.float32)
    raw = jnp.exp(-math.pi * offsets * offsets / (2.0 * LS * LS))
    return (raw / jnp.sqrt(jnp.sum(raw * raw))).astype(jnp.bfloat16)


def band_matrix(rows, taps):
    width = taps.shape[0]
    distance = jnp.arange(rows + width - 1)[None, :] - jnp.arange(rows)[:, None]
    picks = distance[:, :, None] == jnp.arange(width)[None, None, :]
    return jnp.sum(jnp.where(picks, taps.astype(jnp.float32), 0.0), axis=2).astype(jnp.bfloat16)


def filter_last(padded, taps):
    width = taps.shape[0]
    length = padded.shape[-1] - width + 1
    block = math.gcd(length, 128)
    weights = band_matrix(block, taps)
    windows = jnp.stack(
        [
            lax.slice_in_dim(padded, start, start + block + width - 1, axis=padded.ndim - 1)
            for start in range(0, length, block)
        ],
        axis=-2,
    )
    result = jnp.einsum("...kw,bw->...kb", windows, weights, preferred_element_type=jnp.float32)
    return result.reshape(result.shape[:-2] + (length,))


def filter_rows(padded, taps):
    rows = padded.shape[2] - taps.shape[0] + 1
    weights = band_matrix(rows, taps)
    return jnp.einsum("ij,pcjz->pciz", weights, padded, preferred_element_type=jnp.float32)


def cholesky_cells(stress):
    first_diag = jnp.sqrt(stress[0])
    second_low = stress[1] / first_diag
    second_diag = jnp.sqrt(stress[2] - second_low * second_low)
    third_low = stress[3] / first_diag
    third_mid = (stress[4] - second_low * third_low) / second_diag
    third_diag = jnp.sqrt(stress[5] - third_low * third_low - third_mid * third_mid)
    return (first_diag, second_low, second_diag, third_low, third_mid, third_diag)


def velocity_of(state, factors, mean_inflow):
    first_diag, second_low, second_diag, third_low, third_mid, third_diag = factors
    return jnp.stack(
        [
            mean_inflow + first_diag * state[0],
            second_low * state[0] + second_diag * state[1],
            third_low * state[0] + third_mid * state[1] + third_diag * state[2],
        ]
    )


def march(current, courant, velocity):
    upstream = jnp.concatenate([velocity[:, None], current[:, :-1]], axis=1)
    return (1.0 - courant) * current + courant * upstream


def tile_chain(filtered, stress, timescale, mean_inflow, courant, prior_state, field):
    decay = jnp.exp(-math.pi / (2.0 * timescale))
    gain = jnp.sqrt(1.0 - decay * decay)
    factors = cholesky_cells(stress)

    def advance(carry, plane):
        state, current = carry
        state = decay * state + gain * plane
        velocity = velocity_of(state, factors, mean_inflow)
        return ((state, march(current, courant, velocity)), velocity.astype(jnp.bfloat16))

    (state, result), inflow = lax.scan(advance, (prior_state, field), filtered)
    return (inflow, result)


def body(noise, stress, timescale, mean_inflow, courant, prior_state, field):
    taps = filter_taps()
    flipped = jnp.swapaxes(noise, 2, 3)
    tiles = lax.all_to_all(
        lax.all_to_all(flipped, "tile", split_axis=2, concat_axis=3, tiled=True),
        "grp",
        split_axis=3,
        concat_axis=0,
        tiled=True,
    )
    banded = padded_2(tiles, (("grp", 3),), FW, False)
    widened = padded_2(banded, (("tile", 2),), FW, True)
    span = filter_rows(widened, taps).astype(jnp.bfloat16)
    filtered = filter_last(span, taps)
    inflow, result = tile_chain(
        filtered, stress, timescale, mean_inflow, courant, prior_state, field
    )
    return (inflow, result)


def solution(mesh):
    placed = (
        P("grp", None, "tile", None),
        P(None, "tile", "grp"),
        P("tile", "grp"),
        P("tile", "grp"),
        P("tile", "grp"),
        P(None, "tile", "grp"),
        P(None, None, "tile", "grp"),
    )
    return jax.shard_map(
        body,
        mesh=mesh,
        in_specs=placed,
        out_specs=(P(None, None, "tile", "grp"), P(None, None, "tile", "grp")),
        check_vma=False,
    )
```

profile of v0, /device:TPU:63, one launch (start us, length us, event | category | flops | bytes accessed | tf_op | source)
XLA Modules:
  0.0 310.5 jit_solution(12647594609920412347)
XLA Ops:
  0.6 1.9 copy-done.7
  2.5 7.1 %copy.41 = bf16[4,3,64,2048]{2,0,1,3:T(4,128)(2,1)} copy(bf16[4,3,64,2048]{3,2,1,0:T(8,128)(2,1)S(1)} %copy-done.7) | data formatting | bytes 6291456 | tf_op args[0]
  9.6 7.7 %bitcast_bitcast_fusion = bf16[2048,3,4,64]{3,2,1,0:T(4,128)(2,1)} fusion(bf16[4,3,64,2048]{2,0,1,3:T(4,128)(2,1)} %copy.41), kind=kLoop, calls=%fused_computation.73 | loop fusion | bytes 6291456
  17.3 7.5 %reshape.107 = bf16[32,2,24576]{2,1,0:T(2,128)(2,1)S(1)} reshape(bf16[2048,3,4,64]{3,2,1,0:T(4,128)(2,1)} %bitcast_bitcast_fusion) | data formatting | bytes 6291456
  24.8 43.9 %all_to_all.36 = bf16[32,2,24576]{2,1,0:T(2,128)(2,1)} all-to-all(bf16[32,2,24576]{2,1,0:T(2,128)(2,1)S(1)} %reshape.107), channel_id=1, replica_groups=mesh['grp'=4,'tile'=32] {'tile'}, dimensions={0} | all-to-all | bytes 6291456 | tf_op jit(solution)/shard_map/all_to_all | solution.py:104
  68.7 8.7 %reshape.108 = bf16[2048,3,4,64]{3,2,1,0:T(4,128)(2,1)} reshape(bf16[32,2,24576]{2,1,0:T(2,128)(2,1)} %all_to_all.36) | data formatting | bytes 6291456
  77.4 9.5 %copy.65 = bf16[4,3,32,64,64]{4,2,3,1,0:T(8,128)(2,1)} copy(bf16[4,3,32,64,64]{4,0,1,3,2:T(4,128)(2,1)} %bitcast.127) | data formatting | bytes 6291456 | tf_op jit(solution)/shard_map/all_to_all | solution.py:104
  86.9 11.8 %copy.54 = bf16[4,3,64,32,64]{2,0,1,4,3:T(4,128)(2,1)} copy(bf16[4,3,64,32,64]{4,3,2,1,0:T(8,128)(2,1)} %bitcast.128) | data formatting | bytes 6291456 | tf_op jit(solution)/shard_map/all_to_all | solution.py:104
  98.7 7.7 %reshape.109 = bf16[4,2,196608]{2,1,0:T(2,128)(2,1)} reshape(bf16[2048,3,4,64]{3,2,1,0:T(4,128)(2,1)} %bitcast.129) | data formatting | bytes 6291456
  106.5 5.0 %all-to-all-start.1 = ((bf16[4,2,196608]{2,1,0:T(2,128)(2,1)}), bf16[4,2,196608]{2,1,0:T(2,128)(2,1)S(1)}, u32[]{:S(2)}, u32[]{:S(2)}) async-start(bf16[4,2,196608]{2,1,0:T(2,128)(2,1)} %reshape.109), calls=%async_computation.1 | async-start | bytes 6291456 | tf_op jit(solution)/shard_map/all_to_all | solution.py:103
  112.9 2.2 fusion.24
  115.8 1.6 fusion.26
  117.4 30.1 %all-to-all-done.1 = bf16[4,2,196608]{2,1,0:T(2,128)(2,1)S(1)} async-done(((bf16[4,2,196608]{2,1,0:T(2,128)(2,1)}), bf16[4,2,196608]{2,1,0:T(2,128)(2,1)S(1)}, u32[]{:S(2)}, u32[]{:S(2)}) %all-to-all-start.1) | async-done | bytes 3145760 | tf_op jit(solution)/shard_map/all_to_all | solution.py:103
  147.5 5.3 %reshape.110 = bf16[2048,3,4,64]{3,2,1,0:T(4,128)(2,1)} reshape(bf16[4,2,196608]{2,1,0:T(2,128)(2,1)S(1)} %all-to-all-done.1) | data formatting | bytes 6291456
  152.8 8.3 %copy.45 = bf16[4,4,3,64,512]{4,3,2,1,0:T(8,128)(2,1)S(1)} copy(bf16[4,4,3,64,512]{3,1,2,4,0:T(4,128)(2,1)} %bitcast.130) | data formatting | bytes 6291456 | tf_op jit(solution)/shard_map/all_to_all | solution.py:103
  161.1 1.5 fusion.38
  162.6 1.5 copy.46
  164.1 1.5 copy.47
  165.7 3.1 collective-permute-start.1
  168.8 2.4 collective-permute-start
  171.3 2.3 collective-permute-done
  176.1 1.8 pad_maximum_fusion.3
  177.9 5.7 %collective-permute-start.2 = (bf16[16,3,4,520]{3,2,1,0:T(4,128)(2,1)S(1)}, bf16[16,3,4,520]{3,2,1,0:T(4,128)(2,1)S(1)}, u32[]{:S(2)}, u32[]{:S(2)}) collective-permute-start(bf16[16,3,4,520]{3,2,1,0:T(4,128)(2,1)S(1)} %get-tuple-element.126), channel_id=1, source_target_pairs={{0,1},{1,2},{2,3},{3,4},{4,5},{5,6},{6,7},{7,8},{8,9},{9,10},{10,1... | collective-permute-start | bytes 599048 | tf_op jit(solution)/shard_map/ppermute | solution.py:18
  183.6 1.6 sqrt_bitcast_fusion
  185.2 1.5 collective-permute-done.2
  186.7 5.8 %collective-permute-done.3 = bf16[16,3,4,520]{3,2,1,0:T(4,128)(2,1)S(1)} collective-permute-done((bf16[16,3,4,520]{3,2,1,0:T(4,128)(2,1)S(1)}, bf16[16,3,4,520]{3,2,1,0:T(4,128)(2,1)S(1)}, u32[]{:S(2)}, u32[]{:S(2)}) %collective-permute-start.3) | collective-permute-done | bytes 199712 | tf_op jit(solution)/shard_map/ppermute | solution.py:19
  192.5 4.2 %convert_bitcast_fusion.3 = bf16[16,3,64,520]{3,2,1,0:T(8,128)(2,1)S(1)} fusion(bf16[16,3,4,520]{3,2,1,0:T(4,128)(2,1)S(1)} %collective-permute-done.3, bf16[16,3,64,4]{3,2,1,0:T(8,128)(2,1)S(1)} %copy-done.6, bf16[16,3,64,512]{3,2,1,0:T(8,128)(2,1)S(1)} %bitcast.133, bf16[16,3,64,4]{3,2,1,0:T(8,128)(2,1)S(1)} %copy-done.5, ...), kind=kOutput, calls=%fused_computation.35 | convolution fusion | flops 249600000 | bytes 6798336 | tf_op jit(solution)/shard_map/ij,pcjz->pciz/dot_general | solution.py:56
  197.6 2.6 fusion.18
  200.2 3.5 %copy.64 = f32[16,3,4,8,8,128]{5,4,2,3,1,0:T(8,128)} copy(f32[16,3,4,8,8,128]{5,4,3,2,1,0:T(8,128)S(1)} %fusion.18) | data formatting | bytes 12582912 | tf_op jit(solution)/shard_map/reshape | solution.py:50
  203.7 105.1 %while.14 = (s32[]{:T(128)}, f32[3,64,512]{2,1,0:T(8,128)S(1)}, f32[3,8,64,512]{3,2,1,0:T(8,128)S(1)}, bf16[16,3,64,512]{3,2,1,0:T(8,128)(2,1)}, f32[64,512]{1,0...) while((s32[]{:T(128)}, f32[3,64,512]{2,1,0:T(8,128)S(1)}, ...), condition=%wide.region_4.5_spmd, body=%wide.region_3.4_spmd.sunk | while | flops 4685826 | bytes 20512960 | solution.py:96
  205.9 1.4 convert_bitcast_fusion.5
  308.8 1.7 copy-done
  (169 shorter events, 108.2 us)
Async XLA Ops:
  0.6 1.9 copy-start.7
  106.5 6.5 %copy-start.8 = (f32[64,512]{1,0:T(8,128)S(1)}, f32[64,512]{1,0:T(8,128)}, u32[]{:S(2)}) copy-start(f32[64,512]{1,0:T(8,128)} %param.11) | copy-start | bytes 393220
  106.5 41.0 %all-to-all-start.1 = ((bf16[4,2,196608]{2,1,0:T(2,128)(2,1)}), bf16[4,2,196608]{2,1,0:T(2,128)(2,1)S(1)}, u32[]{:S(2)}, u32[]{:S(2)}) async-start(bf16[4,2,196608]{2,1,0:T(2,128)(2,1)} %reshape.109), calls=%async_computation.1 | async-start | bytes 6291456 | tf_op jit(solution)/shard_map/all_to_all | solution.py:103
  115.1 0.7 copy-start.4
  165.7 9.2 %collective-permute-start.1 = (bf16[16,3,64,4]{2,0,3,1:T(8,128)(2,1)S(1)}, bf16[16,3,64,4]{2,0,3,1:T(8,128)(2,1)S(1)}, u32[]{:S(2)}, u32[]{:S(2)}) collective-permute-start(bf16[16,3,64,4]{2,0,3,1:T(8,128)(2,1)S(1)} %copy.47), channel_id=1, source_target_pairs={{32,0},{64,32},{96,64},{33,1},{65,33},{97,65},{34,2},{66,34},{98,6... | collective-permute-start | bytes 73736 | tf_op jit(solution)/shard_map/ppermute | solution.py:19
  168.8 4.8 %collective-permute-start = (bf16[16,3,64,4]{2,0,3,1:T(8,128)(2,1)S(1)}, bf16[16,3,64,4]{2,0,3,1:T(8,128)(2,1)S(1)}, u32[]{:S(2)}, u32[]{:S(2)}) collective-permute-start(bf16[16,3,64,4]{2,0,3,1:T(8,128)(2,1)S(1)} %copy.46), channel_id=1, source_target_pairs={{0,32},{32,64},{64,96},{1,33},{33,65},{65,97},{2,34},{34,66},{66,9... | collective-permute-start | bytes 73736 | tf_op jit(solution)/shard_map/ppermute | solution.py:18
  176.1 16.4 %copy-start.5 = (bf16[16,3,64,4]{3,2,1,0:T(8,128)(2,1)S(1)}, bf16[16,3,64,4]{3,2,1,0:T(8,128)(2,1)}, u32[]{:S(2)}) copy-start(bf16[16,3,64,4]{3,2,1,0:T(8,128)(2,1)} %copy.48) | copy-start | bytes 73732
  176.1 16.4 %copy-start.6 = (bf16[16,3,64,4]{3,2,1,0:T(8,128)(2,1)S(1)}, bf16[16,3,64,4]{3,2,1,0:T(8,128)(2,1)}, u32[]{:S(2)}) copy-start(bf16[16,3,64,4]{3,2,1,0:T(8,128)(2,1)} %copy.49) | copy-start | bytes 73732
  177.9 8.8 %collective-permute-start.2 = (bf16[16,3,4,520]{3,2,1,0:T(4,128)(2,1)S(1)}, bf16[16,3,4,520]{3,2,1,0:T(4,128)(2,1)S(1)}, u32[]{:S(2)}, u32[]{:S(2)}) collective-permute-start(bf16[16,3,4,520]{3,2,1,0:T(4,128)(2,1)S(1)} %get-tuple-element.126), channel_id=1, source_target_pairs={{0,1},{1,2},{2,3},{3,4},{4,5},{5,6},{6,7},{7,8},{8,9},{9,10},{10,1... | collective-permute-start | bytes 599048 | tf_op jit(solution)/shard_map/ppermute | solution.py:18
  183.6 8.9 %collective-permute-start.3 = (bf16[16,3,4,520]{3,2,1,0:T(4,128)(2,1)S(1)}, bf16[16,3,4,520]{3,2,1,0:T(4,128)(2,1)S(1)}, u32[]{:S(2)}, u32[]{:S(2)}) collective-permute-start(bf16[16,3,4,520]{3,2,1,0:T(4,128)(2,1)S(1)} %get-tuple-element.127), channel_id=1, source_target_pairs={{1,0},{2,1},{3,2},{4,3},{5,4},{6,5},{7,6},{8,7},{9,8},{10,9},{11,1... | collective-permute-start | bytes 599048 | tf_op jit(solution)/shard_map/ppermute | solution.py:19
  200.2 3.5 %copy-start.1 = (f32[3,8,64,512]{3,2,1,0:T(8,128)S(1)}, f32[3,8,64,512]{3,2,1,0:T(8,128)}, u32[]{:S(2)}) copy-start(f32[3,8,64,512]{3,2,1,0:T(8,128)} %param.15) | copy-start | bytes 9437188
  200.2 3.5 %copy-start.2 = (f32[3,64,512]{2,1,0:T(8,128)S(1)}, f32[3,64,512]{2,1,0:T(8,128)}, u32[]{:S(2)}) copy-start(f32[3,64,512]{2,1,0:T(8,128)} %param.14) | copy-start | bytes 1179652
  207.3 0.9 copy-start.3
  213.8 0.9 copy-start.3
  220.4 0.9 copy-start.3
  227.0 0.9 copy-start.3
  233.6 0.9 copy-start.3
  240.1 0.9 copy-start.3
  246.7 0.9 copy-start.3
  253.3 0.9 copy-start.3
  259.8 0.9 copy-start.3
  266.4 0.9 copy-start.3
  273.0 0.9 copy-start.3
  279.5 0.9 copy-start.3
  286.1 0.9 copy-start.3
  292.7 0.9 copy-start.3
  299.3 0.9 copy-start.3
  305.8 0.9 copy-start.3
  308.8 1.7 copy-start
where the time goes:
time: 313 us; the launch traced here: 310 us
  local copies, waits for them, and re-layouts  105 us (34%)
  other arithmetic  97.3 us (31%)
  blocking collectives  43.9 us (14%)
  waiting for transfers between devices  39.8 us (13%)
  starting transfers between devices  16.1 us (5%)
  matrix products  6.73 us (2%)
    unnamed x22, local copies, waits for them, and re-layouts  48.3 us
    all_to_all x1, blocking collectives, body(): lax.all_to_all(flipped, 'tile', split_axis=2, concat_axis=3, tiled=True)  43.9 us
    all_to_all x1, waiting for transfers between devices, body(): lax.all_to_all(lax.all_to_all(flipped, 'tile', split_axis=2, concat_axis=...  30.1 us
    another operation x16, other arithmetic, velocity_of(): jnp.stack([mean_inflow + first_diag * state[0], second_low * state[0] + s...  22.1 us
    add x16, other arithmetic, march(): return (1.0 - courant) * current + courant * upstream  22.1 us
    all_to_all x2, local copies, waits for them, and re-layouts, body(): lax.all_to_all(flipped, 'tile', split_axis=2, concat_axis=3, tiled=True)  21.3 us
    add x16, other arithmetic, advance(): state = decay * state + gain * plane  20.4 us
    sub x16, other arithmetic, march(): return (1.0 - courant) * current + courant * upstream  14.6 us
  transfers between devices with their start and end apart: 5, of which 4 were waited for; matrix products, arithmetic and copies ran while one was open for 2% of the time, Pallas kernels for 0%

commit v1 on v0

--- a/solution.py
+++ b/solution.py
@@ -100,13 +100,20 @@
 def body(noise, stress, timescale, mean_inflow, courant, prior_state, field):
     taps = filter_taps()
     flipped = jnp.swapaxes(noise, 2, 3)
-    tiles = lax.all_to_all(
-        lax.all_to_all(flipped, "tile", split_axis=2, concat_axis=3, tiled=True),
-        "grp",
-        split_axis=3,
-        concat_axis=0,
-        tiled=True,
-    )
+    array = lax.all_to_all(flipped, "tile", split_axis=2, concat_axis=3, tiled=True)
+    ways, here = (lax.axis_size("grp"), lax.axis_index("grp"))
+    width_2 = array.shape[3] // ways
+    dims = list(array.shape)
+    dims[3] = width_2
+    height = dims[0]
+    dims[0] = height * ways
+    full = jnp.zeros(dims, array.dtype)
+    for mask in range(ways):
+        part = lax.dynamic_slice_in_dim(array, (here ^ mask) * width_2, width_2, axis=3)
+        if mask:
+            part = lax.ppermute(part, "grp", [(d, d ^ mask) for d in range(ways)])
+        full = lax.dynamic_update_slice_in_dim(full, part, (here ^ mask) * height, axis=0)
+    tiles = full
     banded = padded_2(tiles, (("grp", 3),), FW, False)
     widened = padded_2(banded, (("tile", 2),), FW, True)
     span = filter_rows(widened, taps).astype(jnp.bfloat16)

time: 313 us -> 271 us (0.87)
  blocking collectives: 43.9 us -> 0 us
  waiting for transfers between devices: 39.8 us -> 71.2 us
  local copies, waits for them, and re-layouts: 105 us -> 80.3 us
  other arithmetic: 97.3 us -> 83.3 us
  starting transfers between devices: 16.1 us -> 23.6 us
    all_to_all x1 -> x0, blocking collectives: 43.9 us -> none  [body(): lax.all_to_all(flipped, 'tile', split_axis=2, concat_axis=3, tiled=True)]
    ppermute x0 -> x3, waiting for transfers between devices: none -> 28.4 us  [body(): part = lax.ppermute(part, 'grp', [(d, d ^ mask) for d in range(ways)])]
    sub x16, other arithmetic: 14.6 us -> 0.19 us  [march(): return (1.0 - courant) * current + courant * upstream]
    unnamed x22, local copies, waits for them, and re-layouts: 48.3 us -> 35.9 us
    while x32, local copies, waits for them, and re-layouts: 9.15 us -> 0.06 us
    all_to_all x1 -> x0, local copies, waits for them, and re-layouts: 8.27 us -> none  [body(): lax.all_to_all(lax.all_to_all(flipped, 'tile', split_axis=2, concat_axis=...]
    all_to_all x1, waiting for transfers between devices: 30.1 us -> 35.1 us  [body(): lax.all_to_all(flipped, 'tile', split_axis=2, concat_axis=3, tiled=True)]
    dynamic_update_slice x0 -> x3, local copies, waits for them, and re-layouts: none -> 3.63 us  [body(): lax.dynamic_update_slice_in_dim(full, part, (here ^ mask) * height, axis=0)]
  transfers between devices with their start and end apart: 5 -> 8, of which waited for: 4 -> 6; matrix products, arithmetic and copies ran while one was open for 2% -> 4% of each run, Pallas kernels for 0% -> 0%
where the time goes in v1:
time: 271 us; the launch traced here: 267 us
  other arithmetic  83.3 us (31%)
  local copies, waits for them, and re-layouts  80.3 us (30%)
  waiting for transfers between devices  71.2 us (26%)
  starting transfers between devices  23.6 us (9%)
  matrix products  6.74 us (2%)
    unnamed x22, local copies, waits for them, and re-layouts  35.9 us
    all_to_all x1, waiting for transfers between devices, body(): lax.all_to_all(flipped, 'tile', split_axis=2, concat_axis=3, tiled=True)  35.1 us
    ppermute x3, waiting for transfers between devices, body(): part = lax.ppermute(part, 'grp', [(d, d ^ mask) for d in range(ways)])  28.4 us
    another operation x16, other arithmetic, velocity_of(): jnp.stack([mean_inflow + first_diag * state[0], second_low * state[0] + s...  22.1 us
    add x16, other arithmetic, march(): return (1.0 - courant) * current + courant * upstream  22.1 us
    add x16, other arithmetic, advance(): state = decay * state + gain * plane  20.8 us
    all_to_all x2, local copies, waits for them, and re-layouts, body(): lax.all_to_all(flipped, 'tile', split_axis=2, concat_axis=3, tiled=True)  19.2 us
    dynamic_update_slice x16, other arithmetic, tile_chain(): (state, result), inflow = lax.scan(advance, (prior_state, field), filtered)  11.1 us
  transfers between devices with their start and end apart: 8, of which 6 were waited for; matrix products, arithmetic and copies ran while one was open for 4% of the time, Pallas kernels for 0%

profile of v1, /device:TPU:63, one launch (start us, length us, event | category | flops | bytes accessed | tf_op | source)
XLA Modules:
  0.0 267.3 jit_solution(9293722481869099176)
XLA Ops:
  0.6 1.9 copy-done.8
  2.5 7.2 %copy.35 = bf16[4,3,64,2048]{2,0,1,3:T(4,128)(2,1)} copy(bf16[4,3,64,2048]{3,2,1,0:T(8,128)(2,1)S(1)} %copy-done.8) | data formatting | bytes 6291456 | tf_op args[0]
  9.7 7.7 %bitcast_bitcast_fusion = bf16[2048,3,4,64]{3,2,1,0:T(4,128)(2,1)} fusion(bf16[4,3,64,2048]{2,0,1,3:T(4,128)(2,1)} %copy.35), kind=kLoop, calls=%fused_computation.80 | loop fusion | bytes 6291456
  17.4 8.7 %reshape.107 = bf16[32,2,24576]{2,1,0:T(2,128)(2,1)} reshape(bf16[2048,3,4,64]{3,2,1,0:T(4,128)(2,1)} %bitcast_bitcast_fusion) | data formatting | bytes 6291456
  26.2 7.6 %all-to-all-start = ((bf16[32,2,24576]{2,1,0:T(2,128)(2,1)}), bf16[32,2,24576]{2,1,0:T(2,128)(2,1)S(1)}, u32[]{:S(2)}, u32[]{:S(2)}) async-start(bf16[32,2,24576]{2,1,0:T(2,128)(2,1)} %reshape.107), calls=%async_computation | async-start | bytes 6291456 | tf_op jit(solution)/shard_map/all_to_all | solution.py:103
  35.2 35.1 %all-to-all-done = bf16[32,2,24576]{2,1,0:T(2,128)(2,1)S(1)} async-done(((bf16[32,2,24576]{2,1,0:T(2,128)(2,1)}), bf16[32,2,24576]{2,1,0:T(2,128)(2,1)S(1)}, u32[]{:S(2)}, u32[]{:S(2)}) %all-to-all-start) | async-done | bytes 3145760 | tf_op jit(solution)/shard_map/all_to_all | solution.py:103
  70.3 6.2 %reshape.108 = bf16[2048,3,4,64]{3,2,1,0:T(4,128)(2,1)} reshape(bf16[32,2,24576]{2,1,0:T(2,128)(2,1)S(1)} %all-to-all-done) | data formatting | bytes 6291456
  76.4 9.5 %copy.53 = bf16[4,3,32,64,64]{4,2,3,1,0:T(8,128)(2,1)} copy(bf16[4,3,32,64,64]{4,0,1,3,2:T(4,128)(2,1)} %bitcast.121) | data formatting | bytes 6291456 | tf_op jit(solution)/shard_map/all_to_all | solution.py:103
  85.9 9.7 %all_to_all.16 = bf16[4,3,64,2048]{3,2,1,0:T(8,128)(2,1)} reshape(bf16[4,3,64,32,64]{4,3,2,1,0:T(8,128)(2,1)} %bitcast.122) | data formatting | bytes 6291456 | tf_op jit(solution)/shard_map/all_to_all | solution.py:103
  96.0 1.5 copy-done.4
  97.5 1.5 constant_dynamic-slice_fusion
  99.0 2.9 %collective-permute-start.1 = (bf16[4,3,64,512]{3,2,1,0:T(8,128)(2,1)}, bf16[4,3,64,512]{3,2,1,0:T(8,128)(2,1)}, u32[]{:S(2)}, u32[]{:S(2)}) collective-permute-start(bf16[4,3,64,512]{3,2,1,0:T(8,128)(2,1)} %get-tuple-element.135), channel_id=1, source_target_pairs={{0,64},{32,96},{64,0},{96,32},{1,65},{33,97},{65,1},{97,33},{2,66}... | collective-permute-start | bytes 2359304 | tf_op jit(solution)/shard_map/ppermute | solution.py:114
  102.2 2.2 fusion.24
  104.4 1.7 fusion.26
  106.1 11.4 %collective-permute-done = bf16[4,3,64,512]{3,2,1,0:T(8,128)(2,1)} collective-permute-done((bf16[4,3,64,512]{3,2,1,0:T(8,128)(2,1)}, bf16[4,3,64,512]{3,2,1,0:T(8,128)(2,1)}, u32[]{:S(2)}, u32[]{:S(2)}) %collective-permute-start) | collective-permute-done | bytes 786464 | tf_op jit(solution)/shard_map/ppermute | solution.py:114
  118.7 17.0 %collective-permute-done.1 = bf16[4,3,64,512]{3,2,1,0:T(8,128)(2,1)} collective-permute-done((bf16[4,3,64,512]{3,2,1,0:T(8,128)(2,1)}, bf16[4,3,64,512]{3,2,1,0:T(8,128)(2,1)}, u32[]{:S(2)}, u32[]{:S(2)}) %collective-permute-start.1) | collective-permute-done | bytes 786464 | tf_op jit(solution)/shard_map/ppermute | solution.py:114
  138.2 1.5 fusion.38
  139.7 1.5 copy.37
  141.2 2.2 collective-permute-start.3
  143.4 1.5 copy.38
  145.0 4.0 %collective-permute-start.4 = (bf16[16,3,64,4]{2,0,3,1:T(8,128)(2,1)S(1)}, bf16[16,3,64,4]{2,0,3,1:T(8,128)(2,1)S(1)}, u32[]{:S(2)}, u32[]{:S(2)}) collective-permute-start(bf16[16,3,64,4]{2,0,3,1:T(8,128)(2,1)S(1)} %copy.38), channel_id=1, source_target_pairs={{32,0},{64,32},{96,64},{33,1},{65,33},{97,65},{34,2},{66,34},{98,6... | collective-permute-start | bytes 73736 | tf_op jit(solution)/shard_map/ppermute | solution.py:19
  152.0 1.8 pad_maximum_fusion.3
  153.8 6.7 %collective-permute-start.5 = (bf16[16,3,4,520]{3,2,1,0:T(4,128)(2,1)S(1)}, bf16[16,3,4,520]{3,2,1,0:T(4,128)(2,1)S(1)}, u32[]{:S(2)}, u32[]{:S(2)}) collective-permute-start(bf16[16,3,4,520]{3,2,1,0:T(4,128)(2,1)S(1)} %get-tuple-element.126), channel_id=1, source_target_pairs={{0,1},{1,2},{2,3},{3,4},{4,5},{5,6},{6,7},{7,8},{8,9},{9,10},{10,1... | collective-permute-start | bytes 599048 | tf_op jit(solution)/shard_map/ppermute | solution.py:18
  160.5 1.6 sqrt_bitcast_fusion
  162.1 1.6 collective-permute-done.5
  163.6 5.8 %collective-permute-done.6 = bf16[16,3,4,520]{3,2,1,0:T(4,128)(2,1)S(1)} collective-permute-done((bf16[16,3,4,520]{3,2,1,0:T(4,128)(2,1)S(1)}, bf16[16,3,4,520]{3,2,1,0:T(4,128)(2,1)S(1)}, u32[]{:S(2)}, u32[]{:S(2)}) %collective-permute-start.6) | collective-permute-done | bytes 199712 | tf_op jit(solution)/shard_map/ppermute | solution.py:19
  169.4 4.2 %convert_bitcast_fusion.3 = bf16[16,3,64,520]{3,2,1,0:T(8,128)(2,1)S(1)} fusion(bf16[16,3,4,520]{3,2,1,0:T(4,128)(2,1)S(1)} %collective-permute-done.6, bf16[16,3,64,4]{3,2,1,0:T(8,128)(2,1)S(1)} %copy-done.7, bf16[16,3,64,512]{3,2,1,0:T(8,128)(2,1)S(1)} %constant_dynamic-update-slice_fusion, bf16[16,3,64,4]{3,2,1,0:T(8,128)(2,1)S(1)} %copy-done.6, ...), kind=kOutput, calls=%fused_computation.35 | convolution fusion | flops 249600000 | bytes 6798336 | tf_op jit(solution)/shard_map/ij,pcjz->pciz/dot_general | solution.py:56
  174.5 2.6 fusion.18
  177.1 3.5 %copy.52 = f32[16,3,4,8,8,128]{5,4,2,3,1,0:T(8,128)} copy(f32[16,3,4,8,8,128]{5,4,3,2,1,0:T(8,128)S(1)} %fusion.18) | data formatting | bytes 12582912 | tf_op jit(solution)/shard_map/reshape | solution.py:50
  180.6 2.0 broadcast.36
  183.6 82.1 %while.14 = (s32[]{:T(128)}, f32[3,64,512]{2,1,0:T(8,128)S(1)}, f32[3,8,64,512]{3,2,1,0:T(8,128)S(1)}, bf16[16,3,64,512]{3,2,1,0:T(8,128)(2,1)}, f32[64,512]{1,0...) while((s32[]{:T(128)}, f32[3,64,512]{2,1,0:T(8,128)S(1)}, ...), condition=%wide.region_4.5_spmd, body=%wide.region_3.4_spmd.sunk | while | flops 4685826 | bytes 20513460 | solution.py:96
  265.6 1.7 copy-done
  (178 shorter events, 91.3 us)
Async XLA Ops:
  0.6 1.9 copy-start.8
  26.2 44.1 %all-to-all-start = ((bf16[32,2,24576]{2,1,0:T(2,128)(2,1)}), bf16[32,2,24576]{2,1,0:T(2,128)(2,1)S(1)}, u32[]{:S(2)}, u32[]{:S(2)}) async-start(bf16[32,2,24576]{2,1,0:T(2,128)(2,1)} %reshape.107), calls=%async_computation | async-start | bytes 6291456 | tf_op jit(solution)/shard_map/all_to_all | solution.py:103
  95.6 1.9 copy-start.4
  97.5 4.7 %copy-start.9 = (f32[64,512]{1,0:T(8,128)S(1)}, f32[64,512]{1,0:T(8,128)}, u32[]{:S(2)}) copy-start(f32[64,512]{1,0:T(8,128)} %param.11) | copy-start | bytes 393220
  99.0 18.4 %collective-permute-start = (bf16[4,3,64,512]{3,2,1,0:T(8,128)(2,1)}, bf16[4,3,64,512]{3,2,1,0:T(8,128)(2,1)}, u32[]{:S(2)}, u32[]{:S(2)}) collective-permute-start(bf16[4,3,64,512]{3,2,1,0:T(8,128)(2,1)} %get-tuple-element.136), channel_id=1, source_target_pairs={{0,32},{32,0},{64,96},{96,64},{1,33},{33,1},{65,97},{97,65},{2,34}... | collective-permute-start | bytes 2359304 | tf_op jit(solution)/shard_map/ppermute | solution.py:114
  99.0 36.7 %collective-permute-start.1 = (bf16[4,3,64,512]{3,2,1,0:T(8,128)(2,1)}, bf16[4,3,64,512]{3,2,1,0:T(8,128)(2,1)}, u32[]{:S(2)}, u32[]{:S(2)}) collective-permute-start(bf16[4,3,64,512]{3,2,1,0:T(8,128)(2,1)} %get-tuple-element.135), channel_id=1, source_target_pairs={{0,64},{32,96},{64,0},{96,32},{1,65},{33,97},{65,1},{97,33},{2,66}... | collective-permute-start | bytes 2359304 | tf_op jit(solution)/shard_map/ppermute | solution.py:114
  102.0 34.9 %collective-permute-start.2 = (bf16[4,3,64,512]{3,2,1,0:T(8,128)(2,1)}, bf16[4,3,64,512]{3,2,1,0:T(8,128)(2,1)}, u32[]{:S(2)}, u32[]{:S(2)}) collective-permute-start(bf16[4,3,64,512]{3,2,1,0:T(8,128)(2,1)} %get-tuple-element.134), channel_id=1, source_target_pairs={{0,96},{32,64},{64,32},{96,0},{1,97},{33,65},{65,33},{97,1},{2,98}... | collective-permute-start | bytes 2359304 | tf_op jit(solution)/shard_map/ppermute | solution.py:114
  104.4 32.5 %copy-start.5 = (f32[64,512]{1,0:T(8,128)}, f32[64,512]{1,0:T(8,128)S(1)}, u32[]{:S(2)}) copy-start(f32[64,512]{1,0:T(8,128)S(1)} %get-tuple-element.255) | copy-start | bytes 393220
  141.2 7.9 %collective-permute-start.3 = (bf16[16,3,64,4]{2,0,3,1:T(8,128)(2,1)S(1)}, bf16[16,3,64,4]{2,0,3,1:T(8,128)(2,1)S(1)}, u32[]{:S(2)}, u32[]{:S(2)}) collective-permute-start(bf16[16,3,64,4]{2,0,3,1:T(8,128)(2,1)S(1)} %copy.37), channel_id=1, source_target_pairs={{0,32},{32,64},{64,96},{1,33},{33,65},{65,97},{2,34},{34,66},{66,9... | collective-permute-start | bytes 73736 | tf_op jit(solution)/shard_map/ppermute | solution.py:18
  145.0 5.8 %collective-permute-start.4 = (bf16[16,3,64,4]{2,0,3,1:T(8,128)(2,1)S(1)}, bf16[16,3,64,4]{2,0,3,1:T(8,128)(2,1)S(1)}, u32[]{:S(2)}, u32[]{:S(2)}) collective-permute-start(bf16[16,3,64,4]{2,0,3,1:T(8,128)(2,1)S(1)} %copy.38), channel_id=1, source_target_pairs={{32,0},{64,32},{96,64},{33,1},{65,33},{97,65},{34,2},{66,34},{98,6... | collective-permute-start | bytes 73736 | tf_op jit(solution)/shard_map/ppermute | solution.py:19
  152.0 17.4 %copy-start.6 = (bf16[16,3,64,4]{3,2,1,0:T(8,128)(2,1)S(1)}, bf16[16,3,64,4]{3,2,1,0:T(8,128)(2,1)}, u32[]{:S(2)}) copy-start(bf16[16,3,64,4]{3,2,1,0:T(8,128)(2,1)} %copy.39) | copy-start | bytes 73732
  152.0 17.4 %copy-start.7 = (bf16[16,3,64,4]{3,2,1,0:T(8,128)(2,1)S(1)}, bf16[16,3,64,4]{3,2,1,0:T(8,128)(2,1)}, u32[]{:S(2)}) copy-start(bf16[16,3,64,4]{3,2,1,0:T(8,128)(2,1)} %copy.40) | copy-start | bytes 73732
  153.8 9.8 %collective-permute-start.5 = (bf16[16,3,4,520]{3,2,1,0:T(4,128)(2,1)S(1)}, bf16[16,3,4,520]{3,2,1,0:T(4,128)(2,1)S(1)}, u32[]{:S(2)}, u32[]{:S(2)}) collective-permute-start(bf16[16,3,4,520]{3,2,1,0:T(4,128)(2,1)S(1)} %get-tuple-element.126), channel_id=1, source_target_pairs={{0,1},{1,2},{2,3},{3,4},{4,5},{5,6},{6,7},{7,8},{8,9},{9,10},{10,1... | collective-permute-start | bytes 599048 | tf_op jit(solution)/shard_map/ppermute | solution.py:18
  160.5 8.9 %collective-permute-start.6 = (bf16[16,3,4,520]{3,2,1,0:T(4,128)(2,1)S(1)}, bf16[16,3,4,520]{3,2,1,0:T(4,128)(2,1)S(1)}, u32[]{:S(2)}, u32[]{:S(2)}) collective-permute-start(bf16[16,3,4,520]{3,2,1,0:T(4,128)(2,1)S(1)} %get-tuple-element.127), channel_id=1, source_target_pairs={{1,0},{2,1},{3,2},{4,3},{5,4},{6,5},{7,6},{8,7},{9,8},{10,9},{11,1... | collective-permute-start | bytes 599048 | tf_op jit(solution)/shard_map/ppermute | solution.py:19
  177.1 5.5 %copy-start.2 = (f32[3,64,512]{2,1,0:T(8,128)S(1)}, f32[3,64,512]{2,1,0:T(8,128)}, u32[]{:S(2)}) copy-start(f32[3,64,512]{2,1,0:T(8,128)} %param.14) | copy-start | bytes 1179652
  180.6 3.0 %copy-start.1 = (f32[3,8,64,512]{3,2,1,0:T(8,128)S(1)}, f32[3,8,64,512]{3,2,1,0:T(8,128)}, u32[]{:S(2)}) copy-start(f32[3,8,64,512]{3,2,1,0:T(8,128)} %param.15) | copy-start | bytes 9437188
  183.6 2.7 %copy-start.3 = (f32[64,512]{1,0:T(8,128)S(1)}, f32[64,512]{1,0:T(8,128)}, u32[]{:S(2)}) copy-start(f32[64,512]{1,0:T(8,128)} %get-tuple-element.284) | copy-start | bytes 393220 | tf_op jit(solution)/shard_map/while
  188.7 2.7 %copy-start.3 = (f32[64,512]{1,0:T(8,128)S(1)}, f32[64,512]{1,0:T(8,128)}, u32[]{:S(2)}) copy-start(f32[64,512]{1,0:T(8,128)} %get-tuple-element.284) | copy-start | bytes 393220 | tf_op jit(solution)/shard_map/while
  193.8 2.7 %copy-start.3 = (f32[64,512]{1,0:T(8,128)S(1)}, f32[64,512]{1,0:T(8,128)}, u32[]{:S(2)}) copy-start(f32[64,512]{1,0:T(8,128)} %get-tuple-element.284) | copy-start | bytes 393220 | tf_op jit(solution)/shard_map/while
  199.0 2.7 %copy-start.3 = (f32[64,512]{1,0:T(8,128)S(1)}, f32[64,512]{1,0:T(8,128)}, u32[]{:S(2)}) copy-start(f32[64,512]{1,0:T(8,128)} %get-tuple-element.284) | copy-start | bytes 393220 | tf_op jit(solution)/shard_map/while
  204.1 2.7 %copy-start.3 = (f32[64,512]{1,0:T(8,128)S(1)}, f32[64,512]{1,0:T(8,128)}, u32[]{:S(2)}) copy-start(f32[64,512]{1,0:T(8,128)} %get-tuple-element.284) | copy-start | bytes 393220 | tf_op jit(solution)/shard_map/while
  209.2 2.7 %copy-start.3 = (f32[64,512]{1,0:T(8,128)S(1)}, f32[64,512]{1,0:T(8,128)}, u32[]{:S(2)}) copy-start(f32[64,512]{1,0:T(8,128)} %get-tuple-element.284) | copy-start | bytes 393220 | tf_op jit(solution)/shard_map/while
  214.4 2.7 %copy-start.3 = (f32[64,512]{1,0:T(8,128)S(1)}, f32[64,512]{1,0:T(8,128)}, u32[]{:S(2)}) copy-start(f32[64,512]{1,0:T(8,128)} %get-tuple-element.284) | copy-start | bytes 393220 | tf_op jit(solution)/shard_map/while
  219.5 2.7 %copy-start.3 = (f32[64,512]{1,0:T(8,128)S(1)}, f32[64,512]{1,0:T(8,128)}, u32[]{:S(2)}) copy-start(f32[64,512]{1,0:T(8,128)} %get-tuple-element.284) | copy-start | bytes 393220 | tf_op jit(solution)/shard_map/while
  224.6 2.7 %copy-start.3 = (f32[64,512]{1,0:T(8,128)S(1)}, f32[64,512]{1,0:T(8,128)}, u32[]{:S(2)}) copy-start(f32[64,512]{1,0:T(8,128)} %get-tuple-element.284) | copy-start | bytes 393220 | tf_op jit(solution)/shard_map/while
  229.7 2.7 %copy-start.3 = (f32[64,512]{1,0:T(8,128)S(1)}, f32[64,512]{1,0:T(8,128)}, u32[]{:S(2)}) copy-start(f32[64,512]{1,0:T(8,128)} %get-tuple-element.284) | copy-start | bytes 393220 | tf_op jit(solution)/shard_map/while
  234.9 2.7 %copy-start.3 = (f32[64,512]{1,0:T(8,128)S(1)}, f32[64,512]{1,0:T(8,128)}, u32[]{:S(2)}) copy-start(f32[64,512]{1,0:T(8,128)} %get-tuple-element.284) | copy-start | bytes 393220 | tf_op jit(solution)/shard_map/while
  240.0 2.7 %copy-start.3 = (f32[64,512]{1,0:T(8,128)S(1)}, f32[64,512]{1,0:T(8,128)}, u32[]{:S(2)}) copy-start(f32[64,512]{1,0:T(8,128)} %get-tuple-element.284) | copy-start | bytes 393220 | tf_op jit(solution)/shard_map/while
  245.1 2.7 %copy-start.3 = (f32[64,512]{1,0:T(8,128)S(1)}, f32[64,512]{1,0:T(8,128)}, u32[]{:S(2)}) copy-start(f32[64,512]{1,0:T(8,128)} %get-tuple-element.284) | copy-start | bytes 393220 | tf_op jit(solution)/shard_map/while
  250.3 2.7 %copy-start.3 = (f32[64,512]{1,0:T(8,128)S(1)}, f32[64,512]{1,0:T(8,128)}, u32[]{:S(2)}) copy-start(f32[64,512]{1,0:T(8,128)} %get-tuple-element.284) | copy-start | bytes 393220 | tf_op jit(solution)/shard_map/while
  255.4 2.7 %copy-start.3 = (f32[64,512]{1,0:T(8,128)S(1)}, f32[64,512]{1,0:T(8,128)}, u32[]{:S(2)}) copy-start(f32[64,512]{1,0:T(8,128)} %get-tuple-element.284) | copy-start | bytes 393220 | tf_op jit(solution)/shard_map/while
  260.5 2.7 %copy-start.3 = (f32[64,512]{1,0:T(8,128)S(1)}, f32[64,512]{1,0:T(8,128)}, u32[]{:S(2)}) copy-start(f32[64,512]{1,0:T(8,128)} %get-tuple-element.284) | copy-start | bytes 393220 | tf_op jit(solution)/shard_map/while
  (1 other events, 1.7 us)
